TPU v7x, 32 devices: a whole 2x2x4 slice. The times are simulated.
32 devices in a mesh: row: 16 (over z, y, core), col: 2 (over x).
Axes of the slice: x: 2, y: 2, z: 4, core: 2. Of those that a mesh axis runs over, the one named last changes fastest.
Arguments:
- images: bfloat16 [2048, 1024], P(('row', 'col')), as said below
- texts: bfloat16 [2048, 1024], P(('row', 'col')), as said below
- matches: int32 [2048], P('row'), may hold values from 0 to 2047, each once
- logit_scale: float32 [], replicated, may hold values from 20 to 400
Outputs:
- loss: float32 [], replicated
- image_grad: float32 [2048, 1024], P(('row', 'col'))
- text_grad: float32 [2048, 1024], P(('row', 'col'))
Inputs may be any that keep to these rules, and one draw needn't show every extreme that they name: `images`: each row is a float embedding whose entries are not all zero. `texts`: each row is a float embedding of order one. `matches`: a permutation of the 2048 text indices.
All inputs are finite; a program needn't handle non-finite values.
Results may differ from a plain program's by a relative error of at most 0.0015.
The roundings to bfloat16 on the way count: a program that leaves them out, or rounds other values in their place, can miss the bound.
Values may be sent and summed in bfloat16 or wider, within the bound.
A program may use at most 128 MiB of HBM per device.

v0:
```python
import functools

import jax
import jax.numpy as jnp
from jax import lax
from jax.experimental import pallas as pl
from jax.experimental.pallas import tpu as pltpu
from jax.sharding import PartitionSpec as P

EPSILON = 1e-06
MESH = pl.DeviceIdType.MESH


def merged(value, axis, join):
    pieces = jax.tree.map(lambda part: lax.all_gather(part, axis), value)
    head = jax.tree.map(lambda part: part[0], pieces)
    tail = jax.tree.map(lambda part: part[1:], pieces)
    running, _ = lax.scan(lambda running, piece: (join(running, piece), None), head, tail)
    return running


def unit_rows(values):
    wide = values.astype(jnp.float32)
    norms = jnp.sqrt(jnp.sum(wide * wide, axis=1, keepdims=True) + EPSILON)
    return (wide / norms, norms)


def back_unit(unit, norms, grad):
    inner = jnp.sum(unit * grad, axis=1, keepdims=True)
    return (grad - unit * inner) / norms


def combine_stats(first, second):
    top = jnp.maximum(first[0], second[0])
    return (top, first[1] * jnp.exp(first[0] - top) + second[1] * jnp.exp(second[0] - top))


def on_device(images, texts, matches, logit_scale):
    per_dev = images.shape[0]
    n_row = lax.axis_size("row")
    n_col = lax.axis_size("col")
    total = per_dev * n_row * n_col
    col_pos = lax.axis_index("col")
    row_pos = lax.axis_index("row")
    image_unit, image_norm = unit_rows(images)
    text_unit, text_norm = unit_rows(texts)
    image_low = image_unit.astype(jnp.bfloat16)
    text_low = text_unit.astype(jnp.bfloat16)
    image_rows = lax.all_gather(image_low, "col", axis=0, tiled=True)
    half = 0
    stride = 1
    n_img = image_rows.shape[0]

    def scores_of(piece):
        return logit_scale * lax.dot_general(
            piece, image_rows, (((1,), (1,)), ((), ())), preferred_element_type=jnp.float32
        )

    def match_mask(count):
        place = jnp.arange(count, dtype=jnp.int32)
        owner = place // per_dev * stride + half
        text_ids = owner * (n_col * per_dev) + col_pos * per_dev + place % per_dev
        return text_ids[:, None] == matches[None, :]

    piece = lax.all_gather(text_low, "row", axis=0, tiled=True)
    row_max = jnp.full((n_img,), -jnp.inf, jnp.float32)
    row_sum = jnp.zeros((n_img,), jnp.float32)
    scores = scores_of(piece)
    top = jnp.max(scores, axis=0)
    row_sum = row_sum * jnp.exp(row_max - top) + jnp.sum(jnp.exp(scores - top[None, :]), axis=0)
    piece_max = jnp.max(scores, axis=1)
    piece_sum = jnp.sum(jnp.exp(scores - piece_max[:, None]), axis=1)
    col_max = piece_max
    col_sum = piece_sum
    mask = match_mask(piece.shape[0])
    matched = jnp.sum(jnp.where(mask, scores, jnp.float32(0.0)))
    stats = (top, row_sum, col_max, col_sum, matched)
    row_max, row_sum, col_max, col_sum, matched = stats
    row_max, row_sum = merged((row_max, row_sum), "col", combine_stats)
    slot_max = col_max
    slot_sum = col_sum
    slot_max, slot_sum = merged((slot_max, slot_sum), "row", combine_stats)
    col_max = slot_max
    col_sum = slot_sum
    row_lse = row_max + jnp.log(row_sum)
    col_lse = col_max + jnp.log(col_sum)
    own_rows = jnp.sum(
        lax.dynamic_slice_in_dim(row_lse, (half * n_col + col_pos) * per_dev, per_dev, 0)
    )
    own_cols = jnp.sum(lax.dynamic_slice_in_dim(col_lse, row_pos // stride * per_dev, per_dev, 0))
    share = (own_rows + own_cols) / (2.0 * total) - matched / total
    loss = lax.psum(share, ("row", "col"))
    piece = lax.all_gather(text_low, "row", axis=0, tiled=True)
    count = piece.shape[0]
    scores = scores_of(piece)
    mask = match_mask(count).astype(jnp.float32)
    weights = (
        0.5 * jnp.exp(scores - row_lse[None, :]) + 0.5 * jnp.exp(scores - col_lse[:, None]) - mask
    )
    weights = (logit_scale * weights).astype(jnp.bfloat16)
    image_acc = lax.dot_general(
        weights, piece, (((0,), (0,)), ((), ())), preferred_element_type=jnp.float32
    )
    text_piece = jnp.dot(weights, image_rows, preferred_element_type=jnp.float32)
    text_acc = text_piece
    image_acc, text_acc = (image_acc, text_acc)
    image_unit_grad = lax.psum_scatter(image_acc, "col", scatter_dimension=0, tiled=True)
    text_unit_grad = lax.psum_scatter(text_acc, "row", scatter_dimension=0, tiled=True)
    image_grad = back_unit(image_unit, image_norm, image_unit_grad)
    text_grad = back_unit(text_unit, text_norm, text_unit_grad)
    return (loss, image_grad, text_grad)


def fused_kernel(
    n_row, n_col, img_ref, txt_ref, match_ref, scale_ref, loss_ref, gimg_ref, gtxt_ref,
    raw, low, own, sc, ex, wbuf, stat, tile, lsem, ssem, rsem,
):
    per = img_ref.shape[0]
    n_dev = n_row * n_col
    total = per * n_dev
    units = raw.shape[1]
    width = 4 * per
    pair = 2 * per
    row = lax.axis_index("row")
    x = lax.axis_index("col")
    z, y, c = row // 4, (row // 2) % 2, row % 2
    me = row * n_col + x
    scale = scale_ref[0, 0]

    def place(zz, yy, cc, xx):
        return ((zz * 4 + yy * 2 + cc), xx)

    barrier = pltpu.get_barrier_semaphore()
    peers = [(me + k) % n_dev for k in range(1, n_dev)]
    peers = [(p // n_col, p % n_col) for p in peers]
    greet = [(row,1-x),(z*4+(1-y)*2+c,x),(z*4+y*2+1-c,x)]+[(((z+k)%4)*4+y*2+c,x) for k in (1,2,3)]
    for peer in greet:
        pl.semaphore_signal(barrier, inc=1, device_id=peer, device_id_type=MESH)

    inputs = (img_ref, txt_ref)
    kept = [
        pltpu.make_async_copy(inputs[a], raw.at[a, z * 2 + y, c * 2 + x], lsem.at[a])
        for a in range(2)
    ]
    for copy in kept:
        copy.start()
    for a in range(2):
        wide = inputs[a][...].astype(jnp.float32)
        norm = jnp.sqrt(jnp.sum(wide * wide, axis=1, keepdims=True) + EPSILON)
        own[a] = (wide * (1.0 / norm)).astype(jnp.bfloat16)
    for copy in kept:
        copy.wait()
    pl.semaphore_wait(barrier, len(greet))

    copies = []

    def send(src, dst, target):
        k = len(copies)
        copy = pltpu.make_async_remote_copy(
            src_ref=src, dst_ref=dst, send_sem=ssem.at[k], recv_sem=rsem.at[k],
            device_id=target, device_id_type=MESH,
        )
        copy.start()
        copies.append(copy)
        return copy

    def move(a, zz, yy, xx, target):
        ref = raw.at[a, zz * 2 + yy, c * 2 + xx]
        return send(ref, ref, target)

    to_x, to_y = place(z, y, c, 1 - x), place(z, 1 - y, c, x)
    sibling = place(z, y, 1 - c, x)

    def share(zz, yy, xx):
        ref = raw.at[:, zz * 2 + yy, c * 2 + xx]
        return send(ref, ref, sibling)

    def zmate(k):
        low_bit, high_bit = z % 2, z // 2
        if k & 1:
            low_bit = 1 - low_bit
        if k & 2:
            high_bit = 1 - high_bit
        return high_bit * 2 + low_bit

    zs = [zmate(k) for k in (0, 1, 3, 2)]

    def process(zz, yy):
        unit = zz * 2 + yy
        @pl.loop(0, 4)
        def _(b):
            for a in range(2):
                wide = raw[a, unit, b].astype(jnp.float32)
                norm = jnp.sqrt(jnp.sum(wide * wide, axis=1, keepdims=True) + EPSILON)
                rows = pl.ds(pl.multiple_of(unit * width + b * per, per), per)
                low[a, rows, :] = (wide * (1.0 / norm)).astype(jnp.bfloat16)

        rows = pl.ds(pl.multiple_of(unit * width, width), width)
        for a in range(2):
            sc[a, unit] = scale * lax.dot_general(
                own[1 - a], low[a, rows, :], (((1,), (1,)), ((), ())),
                preferred_element_type=jnp.float32,
            )

    lines = [None]
    first, second, third, shares = {}, {}, {}, {}

    def stage1(k):
        if k:
            for copy in lines[k]:
                copy.wait_recv()
        ax = move(0, zs[k], y, x, to_x)
        by = move(1, zs[k], y, x, to_y)
        bx = move(1, zs[k], y, x, to_x)
        ay = move(0, zs[k], y, x, to_y)
        first[k] = (ax, by)
        second[k] = (bx, ay)
        shares[k] = [share(zs[k], y, x)]

    def stage2(k):
        if k == 1:
            return
        ax, by = first[k]
        ax.wait_recv()
        ady = move(0, zs[k], y, 1 - x, to_y)
        by.wait_recv()
        bdx = move(1, zs[k], 1 - y, x, to_x)
        third[k] = (ady, bdx)

    def stage3(k):
        if k == 1:
            for copy in first[k]:
                copy.wait_recv()
        bx, ay = second[k]
        bx.wait_recv()
        shares[k].append(share(zs[k], y, 1 - x))
        ay.wait_recv()
        shares[k].append(share(zs[k], 1 - y, x))

    def stage4(k):
        for copy in third[k]:
            copy.wait_recv()
        if k == 0:
            corner = raw.at[:, z * 2 + 1 - y, c * 2 + 1 - x]
            third[1] = (send(corner, corner, place(zs[1], y, c, x)),)
        shares[k].append(share(zs[k], 1 - y, 1 - x))

    stage1(0)
    for k in range(1, 4):
        lines.append([move(a, z, y, x, place(zs[k], y, c, x)) for a in range(2)])
    stage2(0)
    for k in range(4):
        if k + 1 < 4:
            stage1(k + 1)
        stage3(k)
        shares[k][0].wait_recv()
        shares[k][1].wait_recv()
        process(zs[k], y)
        stage4(k)
        if k + 1 < 4:
            stage2(k + 1)
        shares[k][2].wait_recv()
        shares[k][3].wait_recv()
        process(zs[k], 1 - y)

    lane = lax.broadcasted_iota(jnp.int32, (per, pair), 1)
    sub = lax.broadcasted_iota(jnp.int32, (per, pair), 0)
    eye = lane == sub + x * per
    match_row = match_ref[...].astype(jnp.float32)
    match_own = jnp.sum(jnp.where(eye, match_row, 0.0), axis=1, keepdims=True)
    lses, sums = [None, None], [None, None]
    for a in range(2):
        top = jnp.max(sc[a, 0], axis=1, keepdims=True)
        for u in range(1, units):
            top = jnp.maximum(top, jnp.max(sc[a, u], axis=1, keepdims=True))
        acc = jnp.zeros((per, width), jnp.float32)
        for u in range(units):
            e = jnp.exp(sc[a, u] - top)
            ex[a, u] = e
            acc = acc + e
        sums[a] = jnp.sum(acc, axis=1, keepdims=True)
        lses[a] = top + jnp.log(sums[a])
    unit_lane = lax.broadcasted_iota(jnp.int32, (per, width), 1).astype(jnp.float32)
    hit = jnp.zeros((per, width), jnp.float32)
    for u in range(units):
        hit = hit + jnp.where(unit_lane + float(u * width) == match_own, sc[1, u], 0.0)
    matched = jnp.sum(jnp.sum(hit, axis=1, keepdims=True), axis=0, keepdims=True)

    def as_lanes(column):
        return jnp.sum(jnp.where(eye, column, 0.0), axis=0, keepdims=True)

    here = lax.broadcasted_iota(jnp.int32, (1, pair), 1)
    inside = (here >= x * per) & (here < (x + 1) * per)
    tile[0:1, :] = as_lanes(lses[1])
    tile[1:2, :] = as_lanes(lses[0])
    tile[2:3, :] = jnp.where(inside, match_row, 0.0)
    tile[3:4, :] = jnp.where(here == 0, matched, 0.0)
    tile[4:8, :] = jnp.zeros((4, pair), jnp.float32)
    stat[me] = tile[...]
    news = [send(tile, stat.at[me], peer) for peer in peers]

    for a in range(2):
        half = 0.5 / sums[a]
        for u in range(units):
            part = ex[a, u] * half
            if a == 1:
                part = part - jnp.where(unit_lane + float(u * width) == match_own, 1.0, 0.0)
            ex[a, u] = part

    for copy in news:
        copy.wait_recv()
    blocks = [stat[2 * k] + stat[2 * k + 1] for k in range(n_dev // 2)]
    everyone = blocks[0]
    for block in blocks[1:]:
        everyone = everyone + block
    rows8 = lax.broadcasted_iota(jnp.int32, everyone.shape, 0)
    factor = jnp.where(rows8 < 2, 0.5 / total, jnp.where(rows8 == 3, -1.0 / total, 0.0))
    loss_ref[...] = jnp.sum(
        jnp.sum(everyone * factor, axis=1, keepdims=True), axis=0, keepdims=True
    )
    text_id = (
        lax.broadcasted_iota(jnp.int32, (per, 1), 0) + me * per
    ).astype(jnp.float32)
    for a in (1, 0):
        for u in range(units):
            wide = jnp.concatenate([blocks[2 * u], blocks[2 * u + 1]], axis=1)
            other = wide[1:2, :] if a == 1 else wide[0:1, :]
            value = ex[a, u] + 0.5 * jnp.exp(sc[a, u] - other)
            if a == 0:
                value = value - jnp.where(wide[2:3, :] == text_id, 1.0, 0.0)
            wbuf[a, :, u * width : (u + 1) * width] = (scale * value).astype(jnp.bfloat16)
        grad = jnp.dot(wbuf[a], low[a], preferred_element_type=jnp.float32)
        source, out = (img_ref, gimg_ref) if a == 1 else (txt_ref, gtxt_ref)
        wide = source[...].astype(jnp.float32)
        norm = jnp.sqrt(jnp.sum(wide * wide, axis=1, keepdims=True) + EPSILON)
        inv = 1.0 / norm
        unit = wide * inv
        inner = jnp.sum(unit * grad, axis=1, keepdims=True)
        out[...] = (grad - unit * inner) * inv
    for copy in copies:
        copy.wait_send()


def fused(n_row, n_col, images, texts, matches, logit_scale):
    per, d = images.shape
    n_dev = n_row * n_col
    units = n_dev // 4
    n_sem = 6 + 10 * 4 + n_dev - 1
    vmem = pl.BlockSpec(memory_space=pltpu.VMEM)
    loss, image_grad, text_grad = pl.pallas_call(
        functools.partial(fused_kernel, n_row, n_col),
        out_shape=(
            jax.ShapeDtypeStruct((1, 1), jnp.float32),
            jax.ShapeDtypeStruct((per, d), jnp.float32),
            jax.ShapeDtypeStruct((per, d), jnp.float32),
        ),
        in_specs=[vmem, vmem, vmem, pl.BlockSpec(memory_space=pltpu.SMEM)],
        out_specs=(vmem, vmem, vmem),
        scratch_shapes=[
            pltpu.VMEM((2, units, 4, per, d), jnp.bfloat16),
            pltpu.VMEM((2, units * 4 * per, d), jnp.bfloat16),
            pltpu.VMEM((2, per, d), jnp.bfloat16),
            pltpu.VMEM((2, units, per, 4 * per), jnp.float32),
            pltpu.VMEM((2, units, per, 4 * per), jnp.float32),
            pltpu.VMEM((2, per, units * 4 * per), jnp.bfloat16),
            pltpu.VMEM((n_dev, 8, 2 * per), jnp.float32),
            pltpu.VMEM((8, 2 * per), jnp.float32),
            pltpu.SemaphoreType.DMA((2,)),
            pltpu.SemaphoreType.DMA((n_sem,)),
            pltpu.SemaphoreType.DMA((n_sem,)),
        ],
        compiler_params=pltpu.CompilerParams(
            collective_id=0, has_side_effects=True, vmem_limit_bytes=56 * 1024 * 1024
        ),
    )(images, texts, matches.reshape(1, -1), logit_scale.reshape(1, 1))
    return loss.reshape(()), image_grad, text_grad


def solution(mesh):
    placed = (P(("row", "col"), None), P(("row", "col"), None), P("row"), P())
    n_row, n_col = mesh.shape["row"], mesh.shape["col"]

    def body(images, texts, matches, logit_scale):
        if n_col == 2 and n_row == 16 and matches.shape[0] == 128:
            return fused(n_row, n_col, images, texts, matches, logit_scale)
        return on_device(images, texts, matches, logit_scale)

    return jax.shard_map(
        body,
        mesh=mesh,
        in_specs=placed,
        out_specs=(P(), P(("row", "col"), None), P(("row", "col"), None)),
        check_vma=False,
    )
```

profile of v0, /device:TPU:0, one launch (start us, length us, event | category | flops | bytes accessed | tf_op | source)
XLA Modules:
  0.0 59.1 jit_solution(10487801191524532009)
XLA Ops:
  1.3 53.6 %shard_map.67 = (f32[1,1]{1,0:T(1,128)}, f32[64,1024]{1,0:T(8,128)}, f32[64,1024]{1,0:T(8,128)}) custom-call(bf16[64,1024]{1,0:T(8,128)(2,1)} %img_ref.1, bf16[64,1024]{1,0:T(8,128)(2,1)} %txt_ref.1, s32[1,128]{1,0:T(1,128)} %bitcast.4, f32[1,1]{1,0:T(1,128)} %bitcast.3.scale_ref), custom_call_target="tpu_custom_call" | custom-call | tf_op jit(solution)/shard_map/pallas_call | solution.py:350
  55.5 0.0 copy-start
  55.6 1.7 %copy.12 = f32[64,1024]{1,0:T(8,128)} copy(f32[64,1024]{1,0:T(8,128)} %get-tuple-element.13) | data formatting | bytes 524288
  57.3 0.0 copy-done
  57.3 0.7 %copy.13 = f32[64,1024]{1,0:T(8,128)} copy(f32[64,1024]{1,0:T(8,128)S(1)} %copy-done) | data formatting | bytes 524288
Async XLA Ops:
  55.5 1.7 %copy-start = (f32[64,1024]{1,0:T(8,128)S(1)}, f32[64,1024]{1,0:T(8,128)}, u32[]{:S(2)}) copy-start(f32[64,1024]{1,0:T(8,128)} %get-tuple-element.14) | copy-start | bytes 786436
where the time goes:
time: 59.3 us; the launch traced here: 59.1 us
  Pallas kernels  53.6 us (90%)
  between operations  3.06 us (5%)
  local copies, waits for them, and re-layouts  2.42 us (4%)
    pallas_call x1, Pallas kernels, fused(): pl.pallas_call(functools.partial(fused_kernel, n_row, n_col), out_shape=(...  53.6 us
    unnamed x4, local copies, waits for them, and re-layouts  2.42 us

commit v1 on v0

v1 whole, which is shorter than its diff:
```python
import functools

import jax
import jax.numpy as jnp
from jax import lax
from jax.experimental import pallas as pl
from jax.experimental.pallas import tpu as pltpu
from jax.sharding import PartitionSpec as P

EPSILON = 1e-06
MESH = pl.DeviceIdType.MESH


def merged(value, axis, join):
    pieces = jax.tree.map(lambda part: lax.all_gather(part, axis), value)
    head = jax.tree.map(lambda part: part[0], pieces)
    tail = jax.tree.map(lambda part: part[1:], pieces)
    running, _ = lax.scan(lambda running, piece: (join(running, piece), None), head, tail)
    return running


def unit_rows(values):
    wide = values.astype(jnp.float32)
    norms = jnp.sqrt(jnp.sum(wide * wide, axis=1, keepdims=True) + EPSILON)
    return (wide / norms, norms)


def back_unit(unit, norms, grad):
    inner = jnp.sum(unit * grad, axis=1, keepdims=True)
    return (grad - unit * inner) / norms


def combine_stats(first, second):
    top = jnp.maximum(first[0], second[0])
    return (top, first[1] * jnp.exp(first[0] - top) + second[1] * jnp.exp(second[0] - top))


def on_device(images, texts, matches, logit_scale):
    per_dev = images.shape[0]
    n_row = lax.axis_size("row")
    n_col = lax.axis_size("col")
    total = per_dev * n_row * n_col
    col_pos = lax.axis_index("col")
    row_pos = lax.axis_index("row")
    image_unit, image_norm = unit_rows(images)
    text_unit, text_norm = unit_rows(texts)
    image_low = image_unit.astype(jnp.bfloat16)
    text_low = text_unit.astype(jnp.bfloat16)
    image_rows = lax.all_gather(image_low, "col", axis=0, tiled=True)
    half = 0
    stride = 1
    n_img = image_rows.shape[0]

    def scores_of(piece):
        return logit_scale * lax.dot_general(
            piece, image_rows, (((1,), (1,)), ((), ())), preferred_element_type=jnp.float32
        )

    def match_mask(count):
        place = jnp.arange(count, dtype=jnp.int32)
        owner = place // per_dev * stride + half
        text_ids = owner * (n_col * per_dev) + col_pos * per_dev + place % per_dev
        return text_ids[:, None] == matches[None, :]

    piece = lax.all_gather(text_low, "row", axis=0, tiled=True)
    row_max = jnp.full((n_img,), -jnp.inf, jnp.float32)
    row_sum = jnp.zeros((n_img,), jnp.float32)
    scores = scores_of(piece)
    top = jnp.max(scores, axis=0)
    row_sum = row_sum * jnp.exp(row_max - top) + jnp.sum(jnp.exp(scores - top[None, :]), axis=0)
    piece_max = jnp.max(scores, axis=1)
    piece_sum = jnp.sum(jnp.exp(scores - piece_max[:, None]), axis=1)
    col_max = piece_max
    col_sum = piece_sum
    mask = match_mask(piece.shape[0])
    matched = jnp.sum(jnp.where(mask, scores, jnp.float32(0.0)))
    stats = (top, row_sum, col_max, col_sum, matched)
    row_max, row_sum, col_max, col_sum, matched = stats
    row_max, row_sum = merged((row_max, row_sum), "col", combine_stats)
    slot_max = col_max
    slot_sum = col_sum
    slot_max, slot_sum = merged((slot_max, slot_sum), "row", combine_stats)
    col_max = slot_max
    col_sum = slot_sum
    row_lse = row_max + jnp.log(row_sum)
    col_lse = col_max + jnp.log(col_sum)
    own_rows = jnp.sum(
        lax.dynamic_slice_in_dim(row_lse, (half * n_col + col_pos) * per_dev, per_dev, 0)
    )
    own_cols = jnp.sum(lax.dynamic_slice_in_dim(col_lse, row_pos // stride * per_dev, per_dev, 0))
    share = (own_rows + own_cols) / (2.0 * total) - matched / total
    loss = lax.psum(share, ("row", "col"))
    piece = lax.all_gather(text_low, "row", axis=0, tiled=True)
    count = piece.shape[0]
    scores = scores_of(piece)
    mask = match_mask(count).astype(jnp.float32)
    weights = (
        0.5 * jnp.exp(scores - row_lse[None, :]) + 0.5 * jnp.exp(scores - col_lse[:, None]) - mask
    )
    weights = (logit_scale * weights).astype(jnp.bfloat16)
    image_acc = lax.dot_general(
        weights, piece, (((0,), (0,)), ((), ())), preferred_element_type=jnp.float32
    )
    text_piece = jnp.dot(weights, image_rows, preferred_element_type=jnp.float32)
    text_acc = text_piece
    image_acc, text_acc = (image_acc, text_acc)
    image_unit_grad = lax.psum_scatter(image_acc, "col", scatter_dimension=0, tiled=True)
    text_unit_grad = lax.psum_scatter(text_acc, "row", scatter_dimension=0, tiled=True)
    image_grad = back_unit(image_unit, image_norm, image_unit_grad)
    text_grad = back_unit(text_unit, text_norm, text_unit_grad)
    return (loss, image_grad, text_grad)


def fused_kernel(
    n_row, n_col, img_ref, txt_ref, match_ref, scale_ref, loss_ref, gimg_ref, gtxt_ref,
    raw, low, sc, ex, wbuf, marks, tile, stat, lse, out, qout, qin, sout, sin, part, parts,
    lsem, osem, ssem, rsem,
):
    per = img_ref.shape[0]
    n_dev = n_row * n_col
    total = per * n_dev
    mine = 4 * per
    both = 2 * mine
    row = lax.axis_index("row")
    x = lax.axis_index("col")
    z, y, c = row // 4, (row // 2) % 2, row % 2
    zh, zl = z // 2, z % 2
    scale = scale_ref[0, 0]

    def place(xx, yy, hh, ll, cc):
        return ((hh * 2 + ll) * 4 + yy * 2 + cc, xx)

    def mate(a, k, other=0):
        near, far, cc = k % 2, k // 2, (c + other) % 2
        if a == 0:
            return place((x + near) % 2, y, zh, (zl + far) % 2, cc)
        return place(x, (y + near) % 2, (zh + far) % 2, zl, cc)

    def slot(a, k):
        near, far = k % 2, k // 2
        if a == 0:
            return (zl + far) % 2 * 2 + (x + near) % 2
        return (zh + far) % 2 * 2 + (y + near) % 2

    sibling = mate(0, 0, 1)
    inputs = (img_ref, txt_ref)
    kept = [
        pltpu.make_async_copy(inputs[a], raw.at[a, c * 4 + slot(a, 0)], lsem.at[a])
        for a in range(2)
    ]
    for copy in kept:
        copy.start()
    barrier = pltpu.get_barrier_semaphore()
    greet = [sibling, mate(0, 1), mate(0, 2), mate(0, 3), mate(1, 1), mate(1, 2)]
    for peer in greet:
        pl.semaphore_signal(barrier, inc=1, device_id=peer, device_id_type=MESH)
    marks[c * 2 + zl] = match_ref[...]

    copies = []

    def send(src, dst, target):
        k = len(copies)
        copy = pltpu.make_async_remote_copy(
            src_ref=src, dst_ref=dst, send_sem=ssem.at[k], recv_sem=rsem.at[k],
            device_id=target, device_id_type=MESH,
        )
        copy.start()
        copies.append(copy)
        return copy

    def move(a, k, target):
        ref = raw.at[a, c * 4 + slot(a, k)]
        return send(ref, ref, target)

    def unit_of(a, cc, k):
        piece = cc * 4 + slot(a, k)
        wide = raw[a, piece].astype(jnp.float32)
        norm = jnp.sqrt(jnp.sum(wide * wide, axis=1, keepdims=True) + EPSILON)
        rows = pl.ds(pl.multiple_of(piece * per, per), per)
        low[a, rows, :] = (wide * (1.0 / norm)).astype(jnp.bfloat16)

    pl.semaphore_wait(barrier, len(greet))
    for copy in kept:
        copy.wait()
    got = {}
    got[1, 2] = move(1, 0, mate(1, 2))
    got[0, 1] = move(0, 0, mate(0, 1))
    got[1, 1] = move(1, 0, mate(1, 1))
    got[0, 2] = move(0, 0, mate(0, 2))
    got[0, 3] = move(0, 0, mate(0, 3))
    shared = {(a, 0): move(a, 0, sibling) for a in range(2)}
    ref = match_ref
    mark_far = send(ref, marks.at[c * 2 + zl], mate(0, 2))
    mark_near = send(ref, marks.at[c * 2 + zl], sibling)

    def arrive(a, k):
        got[a, k].wait_recv()
        if (a, k) == (1, 2):
            got[1, 3] = move(1, 2, mate(1, 1))
        shared[a, k] = move(a, k, sibling)

    def from_sibling(a, k):
        shared[a, k].wait_recv()
        unit_of(a, 1 - c, k)

    for a in range(2):
        unit_of(a, c, 0)
    for a in range(2):
        from_sibling(a, 0)
    mark_far.wait_recv()
    far_marks = marks.at[c * 2 + 1 - zl]
    mark_last = send(far_marks, far_marks, sibling)
    arrive(1, 1)
    arrive(0, 1)
    unit_of(1, c, 1)
    arrive(1, 2)
    unit_of(0, c, 1)
    from_sibling(1, 1)
    from_sibling(0, 1)
    unit_of(1, c, 2)
    from_sibling(1, 2)
    arrive(0, 2)
    unit_of(0, c, 2)
    from_sibling(0, 2)
    mark_near.wait_recv()
    mark_last.wait_recv()
    pair = 2 * per
    square = (pair, pair)
    eye = lax.broadcasted_iota(jnp.int32, square, 0) == lax.broadcasted_iota(jnp.int32, square, 1)

    def as_rows(lanes):
        return [
            jnp.sum(
                jnp.where(eye, lanes[:, k * pair : (k + 1) * pair], 0.0), axis=1, keepdims=True
            )
            for k in range(2)
        ]

    def text_ids(shape, dim, base):
        place_ = lax.broadcasted_iota(jnp.int32, shape, dim) + base
        core, unit, item = place_ // mine, place_ // per % 4, place_ % per
        far, near = unit // 2, unit % 2
        return ((((far * 2 + zl) * 4 + near * 2 + core) * 2 + x) * per + item).astype(jnp.float32)

    match_lanes = jnp.concatenate([marks[k].astype(jnp.float32) for k in range(4)], axis=1)
    match_own = jnp.concatenate([marks[c * 2 + k].astype(jnp.float32) for k in range(2)], axis=1)
    match_rows = as_rows(match_own)
    id_lanes = text_ids((1, both), 1, 0)
    id_rows = text_ids((mine, 1), 0, c * mine)
    arrive(0, 3)
    unit_of(0, c, 3)
    arrive(1, 3)
    unit_of(1, c, 3)
    from_sibling(0, 3)
    from_sibling(1, 3)

    own_rows = pl.ds(pl.multiple_of(c * mine, mine), mine)
    news = []
    tops, factor = [None, None], [None, None]
    for a in (1, 0):
        o = 1 - a
        sc[a] = scale * lax.dot_general(
            low[a, own_rows, :], low[o], (((1,), (1,)), ((), ())),
            preferred_element_type=jnp.float32,
        )
        top = jnp.max(sc[a], axis=0, keepdims=True)
        e = jnp.exp(sc[a] - top)
        ex[a] = e
        tops[o] = top
        here = c * 4 + slot(o, 0)
        fields = [top, jnp.sum(e, axis=0, keepdims=True)]
        if o == 0:
            fields.append(
                jnp.sum(jnp.where(id_rows == match_lanes, sc[a], 0.0), axis=0, keepdims=True)
            )
        for k, field in enumerate(fields):
            tile[o, k] = field
            stat[o, here, k] = field
        for k, other in ((3, 1), (3, 0), (2, 1), (2, 0), (1, 1), (1, 0), (0, 1)):
            n = len(fields)
            news.append((o, send(tile.at[o, 0:n], stat.at[o, here, 0:n], mate(o, k, other))))

    lost = []
    for o in (0, 1):
        for owner, copy in news:
            if owner == o:
                copy.wait_recv()
        most = stat[o, 0, 0]
        for k in range(1, 8):
            most = jnp.maximum(most, stat[o, k, 0])
        sums = stat[o, 0, 1] * jnp.exp(stat[o, 0, 0] - most)
        for k in range(1, 8):
            sums = sums + stat[o, k, 1] * jnp.exp(stat[o, k, 0] - most)
        value = most + jnp.log(sums)
        for k in range(2):
            lse[o, k] = value[:, k * mine : (k + 1) * mine]
        factor[o] = 0.5 * jnp.exp(tops[o] - value)
        term = value * (0.5 / total)
        if o == 0:
            hits = stat[0, 0, 2]
            for k in range(1, 8):
                hits = hits + stat[0, k, 2]
            term = term - hits * (1.0 / total)
        lost.append(jnp.sum(term, axis=1, keepdims=True))

    for a in (1, 0):
        o = 1 - a
        columns = as_rows(lse[a, c])
        for k in range(4):
            rows = slice(k * per, (k + 1) * per)
            half = slice(k % 2 * per, (k % 2 + 1) * per)
            value = ex[a, rows, :] * factor[o] + 0.5 * jnp.exp(
                sc[a, rows, :] - columns[k // 2][half]
            )
            if a == 0:
                hit = id_lanes == match_rows[k // 2][half]
            else:
                hit = id_rows[rows] == match_lanes
            value = value - jnp.where(hit, 1.0, 0.0)
            wbuf[a, rows, :] = (scale * value).astype(jnp.bfloat16)

    def grad_of(a, k):
        rows = pl.ds(pl.multiple_of(slot(a, k) * per, per), per)
        return jnp.dot(wbuf[a, rows, :], low[1 - a], preferred_element_type=jnp.float32)

    def pack_send(value, k, target):
        most = jnp.max(jnp.abs(value), axis=0, keepdims=True)
        most = jnp.maximum(most, 1e-30)
        sout[k] = most * (1.0 / 32767.0)
        qout[k] = jnp.round(value * (32767.0 / most)).astype(jnp.int32).astype(jnp.int16)
        return (
            send(qout.at[k], qin.at[k], target),
            send(sout.at[k], sin.at[k], target),
        )

    def unpack(k, pieces):
        for copy in pieces:
            copy.wait_recv()
        return qin[k].astype(jnp.int32).astype(jnp.float32) * sin[k]

    text_diag = pack_send(grad_of(1, 3), 0, mate(1, 1))
    image_diag = pack_send(grad_of(0, 3), 1, mate(0, 3))
    image_far = pack_send(grad_of(0, 2), 2, mate(0, 2))
    image_near = pack_send(grad_of(0, 1), 3, mate(0, 1))
    text_near = pack_send(grad_of(1, 1), 4, mate(1, 1))
    out[1] = grad_of(1, 2)
    text_far = pack_send(out[1] + unpack(0, text_diag), 5, mate(1, 2))

    parts_out = []
    for o in range(2):
        part[o] = jnp.broadcast_to(lost[o], (1, pair))
        parts[o, slot(1 - o, 0)] = part[o]
        for k in (3, 2, 1):
            parts_out.append(
                send(part.at[o], parts.at[o, slot(1 - o, 0)], mate(1 - o, k))
            )

    out[0] = grad_of(0, 0)
    out[1] = grad_of(1, 0)

    def finish(a, k, pieces, last):
        grad = out[a] + unpack(k, pieces)
        if not last:
            out[a] = grad
            return
        wide = raw[a, c * 4 + slot(a, 0)].astype(jnp.float32)
        norm = jnp.sqrt(jnp.sum(wide * wide, axis=1, keepdims=True) + EPSILON)
        inv = 1.0 / norm
        unit = wide * inv
        inner = jnp.sum(unit * grad, axis=1, keepdims=True)
        out[a] = (grad - unit * inner) * inv
        final = pltpu.make_async_copy(out.at[a], (gimg_ref, gtxt_ref)[a], osem.at[a])
        final.start()
        return final

    finish(0, 3, image_near, False)
    finish(1, 4, text_near, False)
    finish(0, 2, image_far, False)
    done = [finish(0, 1, image_diag, True)]
    done.append(finish(1, 5, text_far, True))
    for copy in parts_out:
        copy.wait_recv()
    loss = jnp.zeros((1, 1), jnp.float32)
    for o in range(2):
        for k in range(4):
            loss = loss + parts[o, k][:, 0:1]
    loss_ref[...] = loss
    for copy in copies:
        copy.wait_send()
    for copy in done:
        copy.wait()


def fused(n_row, n_col, images, texts, matches, logit_scale):
    per, d = images.shape
    n_sem = 64
    vmem = pl.BlockSpec(memory_space=pltpu.VMEM)
    anywhere = pl.BlockSpec(memory_space=pl.ANY)
    loss, image_grad, text_grad = pl.pallas_call(
        functools.partial(fused_kernel, n_row, n_col),
        out_shape=(
            jax.ShapeDtypeStruct((1, 1), jnp.float32),
            jax.ShapeDtypeStruct((per, d), jnp.float32),
            jax.ShapeDtypeStruct((per, d), jnp.float32),
        ),
        in_specs=[anywhere, anywhere, vmem, pl.BlockSpec(memory_space=pltpu.SMEM)],
        out_specs=(vmem, anywhere, anywhere),
        scratch_shapes=[
            pltpu.VMEM((2, 8, per, d), jnp.bfloat16),
            pltpu.VMEM((2, 8 * per, d), jnp.bfloat16),
            pltpu.VMEM((2, 4 * per, 8 * per), jnp.float32),
            pltpu.VMEM((2, 4 * per, 8 * per), jnp.float32),
            pltpu.VMEM((2, 4 * per, 8 * per), jnp.bfloat16),
            pltpu.VMEM((4, 1, 2 * per), jnp.int32),
            pltpu.VMEM((2, 3, 1, 8 * per), jnp.float32),
            pltpu.VMEM((2, 8, 3, 1, 8 * per), jnp.float32),
            pltpu.VMEM((2, 2, 1, 4 * per), jnp.float32),
            pltpu.VMEM((2, per, d), jnp.float32),
            pltpu.VMEM((6, per, d), jnp.int16),
            pltpu.VMEM((6, per, d), jnp.int16),
            pltpu.VMEM((6, 1, d), jnp.float32),
            pltpu.VMEM((6, 1, d), jnp.float32),
            pltpu.VMEM((2, 1, 2 * per), jnp.float32),
            pltpu.VMEM((2, 4, 1, 2 * per), jnp.float32),
            pltpu.SemaphoreType.DMA((2,)),
            pltpu.SemaphoreType.DMA((2,)),
            pltpu.SemaphoreType.DMA((n_sem,)),
            pltpu.SemaphoreType.DMA((n_sem,)),
        ],
        compiler_params=pltpu.CompilerParams(
            collective_id=0, has_side_effects=True, vmem_limit_bytes=56 * 1024 * 1024
        ),
    )(images, texts, matches.reshape(1, -1), logit_scale.reshape(1, 1))
    return loss.reshape(()), image_grad, text_grad


def solution(mesh):
    placed = (P(("row", "col"), None), P(("row", "col"), None), P("row"), P())
    n_row, n_col = mesh.shape["row"], mesh.shape["col"]

    def body(images, texts, matches, logit_scale):
        if n_col == 2 and n_row == 16 and matches.shape[0] == 128:
            return fused(n_row, n_col, images, texts, matches, logit_scale)
        return on_device(images, texts, matches, logit_scale)

    return jax.shard_map(
        body,
        mesh=mesh,
        in_specs=placed,
        out_specs=(P(), P(("row", "col"), None), P(("row", "col"), None)),
        check_vma=False,
    )
```

time: 59.3 us -> 47 us (0.79)
  Pallas kernels: 53.6 us -> 41.4 us
    pallas_call x1, Pallas kernels: 53.6 us -> 41.4 us  [fused(): pl.pallas_call(functools.partial(fused_kernel, n_row, n_col), out_shape=(...]
where the time goes in v1:
time: 47 us; the launch traced here: 46.8 us
  Pallas kernels  41.4 us (88%)
  between operations  3.06 us (7%)
  local copies, waits for them, and re-layouts  2.42 us (5%)
    pallas_call x1, Pallas kernels, fused(): pl.pallas_call(functools.partial(fused_kernel, n_row, n_col), out_shape=(...  41.4 us
    unnamed x4, local copies, waits for them, and re-layouts  2.42 us

profile of v1, /device:TPU:0, one launch (start us, length us, event | category | flops | bytes accessed | tf_op | source)
XLA Modules:
  0.0 46.8 jit_solution(101011936851487061)
XLA Ops:
  1.3 41.4 %shard_map.67 = (f32[1,1]{1,0:T(1,128)}, f32[64,1024]{1,0:T(8,128)}, f32[64,1024]{1,0:T(8,128)}) custom-call(bf16[64,1024]{1,0:T(8,128)(2,1)} %img_ref.1, bf16[64,1024]{1,0:T(8,128)(2,1)} %txt_ref.1, s32[1,128]{1,0:T(1,128)} %bitcast.4, f32[1,1]{1,0:T(1,128)} %bitcast.3.scale_ref), custom_call_target="tpu_custom_call" | custom-call | tf_op jit(solution)/shard_map/pallas_call | solution.py:399
  43.3 0.0 copy-start
  43.3 1.7 %copy.12 = f32[64,1024]{1,0:T(8,128)} copy(f32[64,1024]{1,0:T(8,128)} %get-tuple-element.13) | data formatting | bytes 524288
  45.0 0.0 copy-done
  45.0 0.7 %copy.13 = f32[64,1024]{1,0:T(8,128)} copy(f32[64,1024]{1,0:T(8,128)S(1)} %copy-done) | data formatting | bytes 524288
Async XLA Ops:
  43.3 1.7 %copy-start = (f32[64,1024]{1,0:T(8,128)S(1)}, f32[64,1024]{1,0:T(8,128)}, u32[]{:S(2)}) copy-start(f32[64,1024]{1,0:T(8,128)} %get-tuple-element.14) | copy-start | bytes 786436

commit v2 on v1

--- a/solution.py
+++ b/solution.py
@@ -113,8 +113,8 @@
 
 def fused_kernel(
     n_row, n_col, img_ref, txt_ref, match_ref, scale_ref, loss_ref, gimg_ref, gtxt_ref,
-    raw, low, sc, ex, wbuf, marks, tile, stat, lse, out, qout, qin, sout, sin, part, parts,
-    lsem, osem, ssem, rsem,
+    raw, low, sc, ex, cols, marks, tile, stat, lse, out, qout, qin, sout, sin, part, parts,
+    scalar, lsem, ssem, rsem,
 ):
     per = img_ref.shape[0]
     n_dev = n_row * n_col
@@ -125,7 +125,6 @@
     x = lax.axis_index("col")
     z, y, c = row // 4, (row // 2) % 2, row % 2
     zh, zl = z // 2, z % 2
-    scale = scale_ref[0, 0]
 
     def place(xx, yy, hh, ll, cc):
         return ((hh * 2 + ll) * 4 + yy * 2 + cc, xx)
@@ -142,11 +141,14 @@
             return (zl + far) % 2 * 2 + (x + near) % 2
         return (zh + far) % 2 * 2 + (y + near) % 2
 
+    chunks, late, halves, near_first = 4, True, 2, False
     sibling = mate(0, 0, 1)
     inputs = (img_ref, txt_ref)
     kept = [
-        pltpu.make_async_copy(inputs[a], raw.at[a, c * 4 + slot(a, 0)], lsem.at[a])
-        for a in range(2)
+        pltpu.make_async_copy(inputs[1], raw.at[1, c * 4 + slot(1, 0)], lsem.at[1]),
+        pltpu.make_async_copy(inputs[0], raw.at[0, c * 4 + slot(0, 0)], lsem.at[0]),
+        pltpu.make_async_copy(match_ref, marks.at[c * 2 + zl], lsem.at[2]),
+        pltpu.make_async_copy(scale_ref, scalar, lsem.at[3]),
     ]
     for copy in kept:
         copy.start()
@@ -154,7 +156,6 @@
     greet = [sibling, mate(0, 1), mate(0, 2), mate(0, 3), mate(1, 1), mate(1, 2)]
     for peer in greet:
         pl.semaphore_signal(barrier, inc=1, device_id=peer, device_id_type=MESH)
-    marks[c * 2 + zl] = match_ref[...]
 
     copies = []
 
@@ -168,8 +169,10 @@
         copies.append(copy)
         return copy
 
-    def move(a, k, target):
+    def move(a, k, target, chunk=None):
         ref = raw.at[a, c * 4 + slot(a, k)]
+        if chunk is not None:
+            ref = ref.at[pl.ds(chunk * (per // chunks), per // chunks)]
         return send(ref, ref, target)
 
     def unit_of(a, cc, k):
@@ -179,45 +182,69 @@
         rows = pl.ds(pl.multiple_of(piece * per, per), per)
         low[a, rows, :] = (wide * (1.0 / norm)).astype(jnp.bfloat16)
 
-    pl.semaphore_wait(barrier, len(greet))
+    with jax.named_scope("enter"):
+        pl.semaphore_wait(barrier, len(greet))
     for copy in kept:
         copy.wait()
-    got = {}
-    got[1, 2] = move(1, 0, mate(1, 2))
+    scale = scalar[0, 0]
+    match_ref = marks.at[c * 2 + zl]
+    mark_far = send(match_ref, marks.at[c * 2 + zl], mate(0, 2))
+    mark_near = send(match_ref, marks.at[c * 2 + zl], sibling)
+    got, shared = {}, {}
+    far = [move(1, 0, mate(1, 2), h) for h in range(chunks)]
     got[0, 1] = move(0, 0, mate(0, 1))
     got[1, 1] = move(1, 0, mate(1, 1))
     got[0, 2] = move(0, 0, mate(0, 2))
-    got[0, 3] = move(0, 0, mate(0, 3))
-    shared = {(a, 0): move(a, 0, sibling) for a in range(2)}
-    ref = match_ref
-    mark_far = send(ref, marks.at[c * 2 + zl], mate(0, 2))
-    mark_near = send(ref, marks.at[c * 2 + zl], sibling)
+    if not late:
+        got[0, 3] = move(0, 0, mate(0, 3))
+    for a in range(2):
+        shared[a, 0] = [move(a, 0, sibling)]
 
     def arrive(a, k):
-        got[a, k].wait_recv()
-        if (a, k) == (1, 2):
-            got[1, 3] = move(1, 2, mate(1, 1))
-        shared[a, k] = move(a, k, sibling)
+        with jax.named_scope(f"get{a}{k}"):
+            got[a, k].wait_recv()
+        shared[a, k] = [move(a, k, sibling)]
+
+    corner = []
+    shared[1, 2], shared[1, 3] = [], []
+
+    def relay(h):
+        with jax.named_scope(f"far{h}"):
+            far[h].wait_recv()
+        corner.append(move(1, 2, mate(1, 1), h))
+        shared[1, 2].append(move(1, 2, sibling, h))
+
+    def arrive_corner(h):
+        with jax.named_scope(f"corner{h}"):
+            corner[h].wait_recv()
+        shared[1, 3].append(move(1, 3, sibling, h))
 
     def from_sibling(a, k):
-        shared[a, k].wait_recv()
+        for copy in shared[a, k]:
+            with jax.named_scope(f"share{a}{k}"):
+                copy.wait_recv()
         unit_of(a, 1 - c, k)
 
     for a in range(2):
         unit_of(a, c, 0)
     for a in range(2):
         from_sibling(a, 0)
-    mark_far.wait_recv()
-    far_marks = marks.at[c * 2 + 1 - zl]
-    mark_last = send(far_marks, far_marks, sibling)
     arrive(1, 1)
+    relay(0)
+    if late:
+        got[0, 3] = move(0, 0, mate(0, 3))
     arrive(0, 1)
     unit_of(1, c, 1)
-    arrive(1, 2)
+    for h in range(1, chunks):
+        relay(h)
     unit_of(0, c, 1)
     from_sibling(1, 1)
     from_sibling(0, 1)
     unit_of(1, c, 2)
+    with jax.named_scope("mark_far"):
+        mark_far.wait_recv()
+    far_marks = marks.at[c * 2 + 1 - zl]
+    mark_last = send(far_marks, far_marks, sibling)
     from_sibling(1, 2)
     arrive(0, 2)
     unit_of(0, c, 2)
@@ -244,12 +271,16 @@
 
     match_lanes = jnp.concatenate([marks[k].astype(jnp.float32) for k in range(4)], axis=1)
     match_own = jnp.concatenate([marks[c * 2 + k].astype(jnp.float32) for k in range(2)], axis=1)
-    match_rows = as_rows(match_own)
+    for k, part_rows in enumerate(as_rows(match_own)):
+        for h in range(2):
+            cols[2, 2 * k + h] = part_rows[h * per : (h + 1) * per]
     id_lanes = text_ids((1, both), 1, 0)
     id_rows = text_ids((mine, 1), 0, c * mine)
+    for h in range(chunks - 1):
+        arrive_corner(h)
     arrive(0, 3)
     unit_of(0, c, 3)
-    arrive(1, 3)
+    arrive_corner(chunks - 1)
     unit_of(1, c, 3)
     from_sibling(0, 3)
     from_sibling(1, 3)
@@ -284,7 +315,8 @@
     for o in (0, 1):
         for owner, copy in news:
             if owner == o:
-                copy.wait_recv()
+                with jax.named_scope(f"stat{o}"):
+                    copy.wait_recv()
         most = stat[o, 0, 0]
         for k in range(1, 8):
             most = jnp.maximum(most, stat[o, k, 0])
@@ -304,47 +336,73 @@
         lost.append(jnp.sum(term, axis=1, keepdims=True))
 
     for a in (1, 0):
-        o = 1 - a
-        columns = as_rows(lse[a, c])
-        for k in range(4):
-            rows = slice(k * per, (k + 1) * per)
-            half = slice(k % 2 * per, (k % 2 + 1) * per)
-            value = ex[a, rows, :] * factor[o] + 0.5 * jnp.exp(
-                sc[a, rows, :] - columns[k // 2][half]
+        for k, part_rows in enumerate(as_rows(lse[a, c])):
+            for h in range(2):
+                cols[a, 2 * k + h] = part_rows[h * per : (h + 1) * per]
+
+    def grad_of(a, k):
+        unit = slot(a, k)
+        rows = pl.ds(pl.multiple_of(unit * per, per), per)
+        value = ex[a, rows, :] * factor[1 - a] + 0.5 * jnp.exp(sc[a, rows, :] - cols[a, unit])
+        if a == 0:
+            hit = id_lanes == cols[2, unit]
+        else:
+            hit = text_ids((per, 1), 0, c * mine + unit * per) == match_lanes
+        weights = scale * (value - jnp.where(hit, 1.0, 0.0))
+        return jnp.dot(
+            weights.astype(jnp.bfloat16), low[1 - a], preferred_element_type=jnp.float32
+        )
+
+    def pack_send(value, k, target, pieces=1):
+        sent = []
+        size = per // pieces
+        for h in range(pieces):
+            block = value[h * size : (h + 1) * size]
+            most = jnp.maximum(jnp.max(jnp.abs(block), axis=0, keepdims=True), 1e-30)
+            rows = slice(h * size, (h + 1) * size)
+            sout[k, h] = most * (1.0 / 32767.0)
+            qout[k, rows] = jnp.round(block * (32767.0 / most)).astype(jnp.int32).astype(jnp.int16)
+            sent.append(
+                (
+                    send(qout.at[k, rows], qin.at[k, rows], target),
+                    send(sout.at[k, h], sin.at[k, h], target),
+                )
             )
-            if a == 0:
-                hit = id_lanes == match_rows[k // 2][half]
-            else:
-                hit = id_rows[rows] == match_lanes
-            value = value - jnp.where(hit, 1.0, 0.0)
-            wbuf[a, rows, :] = (scale * value).astype(jnp.bfloat16)
-
-    def grad_of(a, k):
-        rows = pl.ds(pl.multiple_of(slot(a, k) * per, per), per)
-        return jnp.dot(wbuf[a, rows, :], low[1 - a], preferred_element_type=jnp.float32)
-
-    def pack_send(value, k, target):
-        most = jnp.max(jnp.abs(value), axis=0, keepdims=True)
-        most = jnp.maximum(most, 1e-30)
-        sout[k] = most * (1.0 / 32767.0)
-        qout[k] = jnp.round(value * (32767.0 / most)).astype(jnp.int32).astype(jnp.int16)
-        return (
-            send(qout.at[k], qin.at[k], target),
-            send(sout.at[k], sin.at[k], target),
+        return sent
+
+    def unpack(k, sent, h=0):
+        size = per // len(sent)
+        for copy in sent[h]:
+            with jax.named_scope(f"part{k}"):
+                copy.wait_recv()
+        rows = slice(h * size, (h + 1) * size)
+        return qin[k, rows].astype(jnp.int32).astype(jnp.float32) * sin[k, h]
+
+    text_diag = pack_send(grad_of(1, 3), 0, mate(1, 1), halves)
+    if near_first:
+        image_near = pack_send(grad_of(0, 1), 3, mate(0, 1))
+        image_far = pack_send(grad_of(0, 2), 2, mate(0, 2))
+        image_diag = pack_send(grad_of(0, 3), 1, mate(0, 3))
+    else:
+        image_diag = pack_send(grad_of(0, 3), 1, mate(0, 3))
+        image_far = pack_send(grad_of(0, 2), 2, mate(0, 2))
+        image_near = pack_send(grad_of(0, 1), 3, mate(0, 1))
+    out[1] = grad_of(1, 2)
+    text_near = pack_send(grad_of(1, 1), 4, mate(1, 1))
+    text_far = []
+    size = per // halves
+    for h in range(halves):
+        rows = slice(h * size, (h + 1) * size)
+        block = out[1, rows] + unpack(0, text_diag, h)
+        most = jnp.maximum(jnp.max(jnp.abs(block), axis=0, keepdims=True), 1e-30)
+        sout[5, h] = most * (1.0 / 32767.0)
+        qout[5, rows] = jnp.round(block * (32767.0 / most)).astype(jnp.int32).astype(jnp.int16)
+        text_far.append(
+            (
+                send(qout.at[5, rows], qin.at[5, rows], mate(1, 2)),
+                send(sout.at[5, h], sin.at[5, h], mate(1, 2)),
+            )
         )
-
-    def unpack(k, pieces):
-        for copy in pieces:
-            copy.wait_recv()
-        return qin[k].astype(jnp.int32).astype(jnp.float32) * sin[k]
-
-    text_diag = pack_send(grad_of(1, 3), 0, mate(1, 1))
-    image_diag = pack_send(grad_of(0, 3), 1, mate(0, 3))
-    image_far = pack_send(grad_of(0, 2), 2, mate(0, 2))
-    image_near = pack_send(grad_of(0, 1), 3, mate(0, 1))
-    text_near = pack_send(grad_of(1, 1), 4, mate(1, 1))
-    out[1] = grad_of(1, 2)
-    text_far = pack_send(out[1] + unpack(0, text_diag), 5, mate(1, 2))
 
     parts_out = []
     for o in range(2):
@@ -358,59 +416,55 @@
     out[0] = grad_of(0, 0)
     out[1] = grad_of(1, 0)
 
-    def finish(a, k, pieces, last):
-        grad = out[a] + unpack(k, pieces)
-        if not last:
-            out[a] = grad
-            return
-        wide = raw[a, c * 4 + slot(a, 0)].astype(jnp.float32)
+    def close(a, rows, grad):
+        wide = raw[a, c * 4 + slot(a, 0), rows].astype(jnp.float32)
         norm = jnp.sqrt(jnp.sum(wide * wide, axis=1, keepdims=True) + EPSILON)
         inv = 1.0 / norm
         unit = wide * inv
         inner = jnp.sum(unit * grad, axis=1, keepdims=True)
-        out[a] = (grad - unit * inner) * inv
-        final = pltpu.make_async_copy(out.at[a], (gimg_ref, gtxt_ref)[a], osem.at[a])
-        final.start()
-        return final
-
-    finish(0, 3, image_near, False)
-    finish(1, 4, text_near, False)
-    finish(0, 2, image_far, False)
-    done = [finish(0, 1, image_diag, True)]
-    done.append(finish(1, 5, text_far, True))
-    for copy in parts_out:
-        copy.wait_recv()
+        (gimg_ref, gtxt_ref)[a][rows] = (grad - unit * inner) * inv
+
+    whole = slice(0, per)
+    out[0] = out[0] + unpack(3, image_near)
+    out[1] = out[1] + unpack(4, text_near)
+    out[0] = out[0] + unpack(2, image_far)
+    close(0, whole, out[0] + unpack(1, image_diag))
+    for h in range(halves):
+        rows = slice(h * size, (h + 1) * size)
+        close(1, rows, out[1, rows] + unpack(5, text_far, h))
+    with jax.named_scope("loss"):
+        for copy in parts_out:
+            copy.wait_recv()
     loss = jnp.zeros((1, 1), jnp.float32)
     for o in range(2):
         for k in range(4):
             loss = loss + parts[o, k][:, 0:1]
-    loss_ref[...] = loss
-    for copy in copies:
-        copy.wait_send()
-    for copy in done:
-        copy.wait()
+    loss_ref[0, 0] = jnp.sum(loss)
+    with jax.named_scope("leave"):
+        for copy in copies:
+            copy.wait_send()
 
 
 def fused(n_row, n_col, images, texts, matches, logit_scale):
     per, d = images.shape
-    n_sem = 64
+    n_sem = 80
     vmem = pl.BlockSpec(memory_space=pltpu.VMEM)
-    anywhere = pl.BlockSpec(memory_space=pl.ANY)
+    hbm = pl.BlockSpec(memory_space=pltpu.HBM)
     loss, image_grad, text_grad = pl.pallas_call(
         functools.partial(fused_kernel, n_row, n_col),
         out_shape=(
-            jax.ShapeDtypeStruct((1, 1), jnp.float32),
-            jax.ShapeDtypeStruct((per, d), jnp.float32),
-            jax.ShapeDtypeStruct((per, d), jnp.float32),
+            pltpu.SMEM((1, 1), jnp.float32),
+            pltpu.VMEM((per, d), jnp.float32),
+            pltpu.VMEM((per, d), jnp.float32),
         ),
-        in_specs=[anywhere, anywhere, vmem, pl.BlockSpec(memory_space=pltpu.SMEM)],
-        out_specs=(vmem, anywhere, anywhere),
+        in_specs=[hbm, hbm, hbm, hbm],
+        out_specs=(pl.BlockSpec(memory_space=pltpu.SMEM), vmem, vmem),
         scratch_shapes=[
             pltpu.VMEM((2, 8, per, d), jnp.bfloat16),
             pltpu.VMEM((2, 8 * per, d), jnp.bfloat16),
             pltpu.VMEM((2, 4 * per, 8 * per), jnp.float32),
             pltpu.VMEM((2, 4 * per, 8 * per), jnp.float32),
-            pltpu.VMEM((2, 4 * per, 8 * per), jnp.bfloat16),
+            pltpu.VMEM((3, 4, per, 1), jnp.float32),
             pltpu.VMEM((4, 1, 2 * per), jnp.int32),
             pltpu.VMEM((2, 3, 1, 8 * per), jnp.float32),
             pltpu.VMEM((2, 8, 3, 1, 8 * per), jnp.float32),
@@ -418,12 +472,12 @@
             pltpu.VMEM((2, per, d), jnp.float32),
             pltpu.VMEM((6, per, d), jnp.int16),
             pltpu.VMEM((6, per, d), jnp.int16),
-            pltpu.VMEM((6, 1, d), jnp.float32),
-            pltpu.VMEM((6, 1, d), jnp.float32),
+            pltpu.VMEM((6, 2, 1, d), jnp.float32),
+            pltpu.VMEM((6, 2, 1, d), jnp.float32),
             pltpu.VMEM((2, 1, 2 * per), jnp.float32),
             pltpu.VMEM((2, 4, 1, 2 * per), jnp.float32),
-            pltpu.SemaphoreType.DMA((2,)),
-            pltpu.SemaphoreType.DMA((2,)),
+            pltpu.SMEM((1, 1), jnp.float32),
+            pltpu.SemaphoreType.DMA((4,)),
             pltpu.SemaphoreType.DMA((n_sem,)),
             pltpu.SemaphoreType.DMA((n_sem,)),
         ],

time: 47 us -> 39.8 us (0.85)
  Pallas kernels: 41.4 us -> 36.4 us
  between operations: 3.06 us -> 1.8 us
  local copies, waits for them, and re-layouts: 2.42 us -> 1.41 us
    pallas_call x1, Pallas kernels: 41.4 us -> 36.4 us  [fused(): pl.pallas_call(functools.partial(fused_kernel, n_row, n_col), out_shape=(...]
    unnamed x4 -> x2, local copies, waits for them, and re-layouts: 2.42 us -> 1.41 us
where the time goes in v2:
time: 39.8 us; the launch traced here: 39.7 us
  Pallas kernels  36.4 us (91%)
  between operations  1.8 us (5%)
  local copies, waits for them, and re-layouts  1.41 us (4%)
    pallas_call x1, Pallas kernels, fused(): pl.pallas_call(functools.partial(fused_kernel, n_row, n_col), out_shape=(...  36.4 us
    unnamed x2, local copies, waits for them, and re-layouts  1.41 us

profile of v2, /device:TPU:0, one launch (start us, length us, event | category | flops | bytes accessed | tf_op | source)
XLA Modules:
  0.0 39.7 jit_solution(9831766780777695236)
XLA Ops:
  1.3 36.4 %shard_map.67 = (f32[1,1]{1,0:T(1,128)S(4)}, f32[64,1024]{1,0:T(8,128)S(1)}, f32[64,1024]{1,0:T(8,128)S(1)}) custom-call(bf16[64,1024]{1,0:T(8,128)(2,1)} %img_ref.1, bf16[64,1024]{1,0:T(8,128)(2,1)} %txt_ref.1, s32[1,128]{1,0:T(1,128)} %bitcast.4, f32[1,1]{1,0:T(1,128)} %bitcast.3.scale_ref), custom_call_target="tpu_custom_call" | custom-call | tf_op jit(solution)/shard_map/pallas_call | solution.py:453
  38.2 0.7 %copy.11 = f32[64,1024]{1,0:T(8,128)} copy(f32[64,1024]{1,0:T(8,128)S(1)} %get-tuple-element.10) | data formatting | bytes 524288
  38.9 0.7 %copy.12 = f32[64,1024]{1,0:T(8,128)} copy(f32[64,1024]{1,0:T(8,128)S(1)} %get-tuple-element.11) | data formatting | bytes 524288
